TPU v7x, 32 devices: a whole 2x2x4 slice. The times are simulated.
32 devices in a mesh: mem: 4 (over z), state: 8 (over y, x, core).
Axes of the slice: x: 2, y: 2, z: 4, core: 2. Of those that a mesh axis runs over, the one named last changes fastest.
Arguments:
- anomalies: bfloat16 [64, 32, 32768], P('mem', None, 'state'), may hold values from -0.75 to 0.75
- alpha: bfloat16 [64, 32, 2048], P('mem', None, 'state'), may hold values from -6 to 6
- basis: bfloat16 [2048, 32768], P(None, 'state'), may hold values from -0.1875 to 0.1875
- gradient: bfloat16 [32, 32768], P(None, 'state'), may hold values from -6 to 6
- vertical_root: float32 [32, 32], replicated, may hold values from -1 to 1
- band_gain: float32 [16], replicated, may hold values from 0.25 to 2
- band: int32 [2048], P('state'), may hold values from 0 to 15
- order: int32 [64], replicated, may hold values from 0 to 63, each once
Outputs:
- increment: float32 [32, 32768], P(None, 'state')
- alpha_grad: float32 [64, 32, 2048], P('mem', None, 'state')
Inputs may be any that keep to these rules, and one draw needn't show every extreme that they name: `order`: a permutation: every member is named by exactly one slot.
All inputs are finite; a program needn't handle non-finite values.
Results may differ from a plain program's by a relative error of at most 0.0029.
Values may be sent and summed in bfloat16 or wider, within the bound.
No kernel may reach another device: no remote copies, remote signals or barrier semaphores. Data moves between devices by JAX's collectives and lax.ppermute only.
A program may use at most 128 MiB of HBM per device.

v0:
```python
import jax
import jax.numpy as jnp
from jax import lax
from jax.sharding import PartitionSpec as P


def on_device(anomalies, alpha, basis, gradient, vertical_root, band_gain, band, order):
    high = lax.Precision.HIGHEST
    mem_count = lax.axis_size("mem")
    mem_rank = lax.axis_index("mem")
    member_dev, levels, columns = anomalies.shape
    mode_rows = alpha.shape[2]
    bands = band_gain.shape[0]
    onehot = (band[:, None] == jnp.arange(bands, dtype=jnp.int32)[None, :]).astype(jnp.float32)
    filter_gain = jnp.sum(onehot * band_gain[None, :], axis=1)
    coef = jnp.einsum("ab,jbk->jak", vertical_root, alpha.astype(jnp.float32), precision=high)
    coef = (coef * filter_gain[None, None, :]).astype(jnp.bfloat16)
    members = mem_rank * member_dev + jnp.arange(member_dev, dtype=jnp.int32)
    select = (order[None, :] == members[:, None]).astype(jnp.bfloat16)
    state_count = lax.axis_size("state")
    gathered = lax.all_gather(coef[None], ("mem", "state"), axis=0, tiled=True)
    blocks = gathered.reshape(mem_count, state_count, member_dev, levels, mode_rows)
    picked = jnp.einsum(
        "imj,msjlc->ilsc",
        select.reshape(member_dev, mem_count, member_dev),
        blocks,
        preferred_element_type=jnp.float32,
    )
    picked = picked.astype(jnp.bfloat16).reshape(member_dev * levels, state_count * mode_rows)
    member_field = jnp.dot(picked, basis, preferred_element_type=jnp.float32)
    partial_value = jnp.sum(
        anomalies.astype(jnp.float32) * member_field.reshape(member_dev, levels, columns), axis=0
    )
    increment = lax.psum(partial_value, "mem")
    weighted = (anomalies.astype(jnp.float32) * gradient.astype(jnp.float32)[None]).astype(
        jnp.bfloat16
    )
    weighted = weighted.reshape(member_dev * levels, columns)
    projected = lax.psum_scatter(
        lax.dot_general(
            basis, weighted, (((1,), (1,)), ((), ())), preferred_element_type=jnp.float32
        ),
        "state",
        scatter_dimension=0,
        tiled=True,
    )
    member_grad = jnp.einsum(
        "ab,kma->mbk",
        vertical_root,
        projected.reshape(mode_rows, member_dev, levels),
        precision=high,
    )
    member_grad = member_grad * filter_gain[None, None, :]
    placed = jnp.einsum("ij,ibk->jbk", select.astype(jnp.float32), member_grad, precision=high)
    outgoing = placed.reshape(mem_count, member_dev, levels, mode_rows)
    incoming = lax.all_to_all(outgoing, "mem", split_axis=0, concat_axis=0, tiled=True)
    alpha_grad = jnp.sum(incoming, axis=0)
    return (increment, alpha_grad)


def solution(mesh):
    return jax.shard_map(
        on_device,
        mesh=mesh,
        in_specs=(
            P("mem", None, "state"),
            P("mem", None, "state"),
            P(None, "state"),
            P(None, "state"),
            P(),
            P(),
            P("state"),
            P(),
        ),
        out_specs=(P(None, "state"), P("mem", None, "state")),
        check_vma=False,
    )
```

profile of v0, /device:TPU:0, one launch (start us, length us, event | category | flops | bytes accessed | tf_op | source)
XLA Modules:
  0.0 206.5 jit_solution(10233362292895392196)
XLA Ops:
  8.0 0.0 copy-start
  8.0 0.0 reduce-scatter.2.cloned.1.call-start
  8.1 1.0 convert_element_type.31
  9.1 3.3 %fusion.3 = bf16[16,32,4096]{2,1,0:T(8,128)(2,1)S(1)} fusion(bf16[16,32,4096]{2,1,0:T(8,128)(2,1)} %param.8, f32[32,4096]{1,0:T(8,128)S(1)} %convert_element_type.31), kind=kLoop, calls=%fused_computation.5 | loop fusion | flops 6291456 | bytes 8912896 | tf_op jit(solution)/shard_map/convert_element_type | solution.py:35
  12.4 13.7 %convolution_bitcast_fusion = f32[2048,512]{0,1:T(8,128)} fusion(bf16[512,4096]{1,0:T(8,128)(2,1)S(1)} %bitcast.44, bf16[2048,4096]{1,0:T(8,128)(2,1)} %param.10), kind=kOutput, calls=%fused_computation.9 | convolution fusion | flops 8589934592 | bytes 25165824 | tf_op jit(solution)/shard_map/dot_general | solution.py:40
  26.2 0.0 reduce-scatter.2.cloned.1.call-update
  26.2 0.0 all-gather.3.cloned.1.call-start
  26.2 0.6 copy-done.3
  26.8 0.0 copy-done.4
  26.8 0.1 select_reduce_fusion
  26.9 0.0 copy-done
  26.9 0.0 copy-done.1
  26.9 1.1 fusion.15
  28.0 0.0 all-gather.3.cloned.1.call-update
  28.0 0.1 eq.38
  28.1 52.4 %reduce-scatter.2.cloned.1.call-done = f32[256,512]{0,1:T(8,128)} async-done(((f32[2048,512]{0,1:T(8,128)}), f32[256,512]{0,1:T(8,128)}) %reduce-scatter.2.cloned.1.call-update) | async-done | bytes 524304 | tf_op jit(solution)/shard_map/reduce_scatter | solution.py:39
  80.5 1.7 fusion.13
  82.2 1.2 fusion.16
  83.3 1.6 copy.30
  84.9 4.6 %all-to-all-start = ((f32[4,16,32,256]{3,1,2,0:T(8,128)}), f32[4,16,32,256]{3,1,2,0:T(8,128)S(1)}, u32[]{:S(2)}, u32[]{:S(2)}) async-start(f32[4,16,32,256]{3,1,2,0:T(8,128)} %copy.30), calls=%async_computation.1 | async-start | bytes 4194304 | tf_op jit(solution)/shard_map/all_to_all | solution.py:56
  89.5 0.0 all-reduce.2.cloned.1.call-start
  89.5 41.0 %all-gather.3.cloned.1.call-done = bf16[512,32,256]{2,1,0:T(8,128)(2,1)} async-done(((bf16[16,32,256]{2,1,0:T(8,128)(2,1)}), bf16[512,32,256]{2,1,0:T(8,128)(2,1)}) %all-gather.3.cloned.1.call-update) | async-done | bytes 8388624 | tf_op jit(solution)/shard_map/all_gather | solution.py:21
  130.5 8.1 %fusion.10 = bf16[16,32,8,256]{3,0,1,2:T(8,128)(2,1)S(1)} fusion(bf16[4,8,16,32,256]{4,3,2,1,0:T(8,128)(2,1)} %bitcast.46, s32[4,16]{1,0:T(4,128)S(1)} %eq.38, s32[16]{0:T(128)S(1)} %iota_add_fusion), kind=kOutput, calls=%fused_computation.10 | convolution fusion | flops 135267328 | bytes 10486080 | tf_op jit(solution)/shard_map/imj,msjlc->ilsc/dot_general | solution.py:23
  138.6 2.5 %copy.27 = bf16[16,32,8,256]{3,2,1,0:T(8,128)(2,1)} copy(bf16[16,32,8,256]{3,0,1,2:T(8,128)(2,1)S(1)} %fusion.10) | data formatting | bytes 4194304 | tf_op jit(solution)/shard_map/convert_element_type | solution.py:29
  141.1 4.2 %dot_general.24 = bf16[16,32,2048]{2,1,0:T(8,128)(2,1)} reshape(bf16[16,32,8,256]{3,2,1,0:T(8,128)(2,1)} %copy.27) | data formatting | bytes 4194304 | tf_op jit(solution)/shard_map/dot_general | solution.py:30
  145.3 14.4 %fusion.2 = f32[32,4096]{1,0:T(8,128)} fusion(bf16[16,32,4096]{2,1,0:T(8,128)(2,1)} %param.8, bf16[16,32,2048]{2,1,0:T(8,128)(2,1)} %dot_general.24, bf16[2048,4096]{1,0:T(8,128)(2,1)} %param.10), kind=kOutput, calls=%fused_computation.4 | convolution fusion | flops 8596094976 | bytes 23592960 | tf_op jit(solution)/shard_map/dot_general | solution.py:30
  159.8 0.0 all-reduce.2.cloned.1.call-update
  159.8 0.0 all-to-all-done
  159.8 0.2 reduce_sum.29
  160.1 1.1 copy.32
  161.2 36.1 %all-reduce.2.cloned.1.call-done = f32[32,4096]{1,0:T(8,128)} async-done(((f32[32,4096]{1,0:T(8,128)}), f32[32,4096]{1,0:T(8,128)}) %all-reduce.2.cloned.1.call-update) | async-done | bytes 524304 | tf_op jit(solution)/shard_map/psum | solution.py:34
  197.2 1.9 copy.47
  (6 shorter events, 0.0 us)
Async XLA Ops:
  8.0 18.9 %copy-start = (bf16[16,32,256]{2,1,0:T(8,128)(2,1)S(1)}, bf16[16,32,256]{2,1,0:T(8,128)(2,1)}, u32[]{:S(2)}) copy-start(bf16[16,32,256]{2,1,0:T(8,128)(2,1)} %param.9) | copy-start | bytes 786436
  8.0 72.5 %reduce-scatter.2.cloned.1.call-start = ((), (), s32[]{:S(2)}) async-start(), calls=%async_computation.3 | async-start | bytes 4718592 | tf_op jit(solution)/shard_map/reduce_scatter | solution.py:39
  26.2 0.7 copy-start.3
  26.2 0.7 copy-start.4
  26.2 0.8 copy-start.1
  26.2 1.9 copy-start.2
  26.2 104.3 %all-gather.3.cloned.1.call-start = ((), (), s32[]{:S(2)}) async-start(), calls=%async_computation.4 | async-start | bytes 8650752 | tf_op jit(solution)/shard_map/all_gather | solution.py:21
  84.9 74.9 %all-to-all-start = ((f32[4,16,32,256]{3,1,2,0:T(8,128)}), f32[4,16,32,256]{3,1,2,0:T(8,128)S(1)}, u32[]{:S(2)}, u32[]{:S(2)}) async-start(f32[4,16,32,256]{3,1,2,0:T(8,128)} %copy.30), calls=%async_computation.1 | async-start | bytes 4194304 | tf_op jit(solution)/shard_map/all_to_all | solution.py:56
  89.5 107.7 %all-reduce.2.cloned.1.call-start = ((), (), s32[]{:S(2)}) async-start(), calls=%async_computation.2 | async-start | bytes 1048576 | tf_op jit(solution)/shard_map/psum | solution.py:34
Sparse Core Ops, SparseCore 0:
  26.3 54.1 reduce-scatter.1
Sparse Core Ops, SparseCore 1:
  30.1 100.3 all-gather.2
  159.9 37.3 all-reduce.1
where the time goes:
time: 207 us
  waiting for transfers between devices  129 us (62%)
  matrix products  40.2 us (19%)
  between operations  15.6 us (8%)
  local copies, waits for them, and re-layouts  11.9 us (6%)
  starting transfers between devices  4.71 us (2%)
  other arithmetic  4.69 us (2%)
    reduce_scatter x1, waiting for transfers between devices, on_device(): lax.psum_scatter(lax.dot_general(basis, weighted, (((1,), (1,)), ((), ())...  52.4 us
    all_gather x1, waiting for transfers between devices, on_device(): gathered = lax.all_gather(coef[None], ('mem', 'state'), axis=0, tiled=True)  41 us
    psum x1, waiting for transfers between devices, on_device(): increment = lax.psum(partial_value, 'mem')  36.1 us
    dot_general x1, matrix products, on_device(): member_field = jnp.dot(picked, basis, preferred_element_type=jnp.float32)  14.4 us
    dot_general x1, matrix products, on_device(): lax.dot_general(basis, weighted, (((1,), (1,)), ((), ())), preferred_elem...  13.7 us
    dot_general x1, matrix products, on_device(): jnp.einsum('imj,msjlc->ilsc', select.reshape(member_dev, mem_count, membe...  8.11 us
    all_to_all x1, starting transfers between devices, on_device(): lax.all_to_all(outgoing, 'mem', split_axis=0, concat_axis=0, tiled=True)  4.62 us
    dot_general x1, local copies, waits for them, and re-layouts, on_device(): member_field = jnp.dot(picked, basis, preferred_element_type=jnp.float32)  4.19 us
  transfers between devices with their start and end apart: 4, of which 3 were waited for; matrix products, arithmetic and copies ran while one was open for 18% of the time, Pallas kernels for 0%

commit v1 on v0

v1 whole, which is shorter than its diff:
```python
import jax
import jax.numpy as jnp
from jax import lax
from jax.experimental import pallas as pl
from jax.experimental.pallas import tpu as pltpu
from jax.sharding import PartitionSpec as P


def project_kernel(rows_ref, anomalies_ref, gradient_ref, basis_ref, given_ref, kept_ref, weighted_ref):
    step = pl.program_id(0)
    levels = gradient_ref.shape[0]

    @pl.when(step == 0)
    def _():
        scale = gradient_ref[...].astype(jnp.float32)
        for member in range(anomalies_ref.shape[0]):
            value = anomalies_ref[member].astype(jnp.float32) * scale
            weighted_ref[member * levels : (member + 1) * levels, :] = value.astype(jnp.bfloat16)

    def sums():
        return lax.dot_general(
            weighted_ref[...], basis_ref[...], (((1,), (1,)), ((), ())), preferred_element_type=jnp.float32
        )

    half = pl.num_programs(0) // 2

    @pl.when(step < half)
    def _():
        given_ref[0] = sums()

    @pl.when(step >= half)
    def _():
        kept_ref[0] = sums()


def project(anomalies, gradient, basis, rows, width):
    members, levels, columns = anomalies.shape
    height, count = members * levels, rows.shape[0]
    half = count // 2
    result = jax.ShapeDtypeStruct((half, height, width), jnp.float32)
    return pl.pallas_call(
        project_kernel,
        grid_spec=pltpu.PrefetchScalarGridSpec(
            num_scalar_prefetch=1,
            grid=(count,),
            in_specs=[
                pl.BlockSpec((members, levels, columns), lambda g, rows: (0, 0, 0)),
                pl.BlockSpec((levels, columns), lambda g, rows: (0, 0)),
                pl.BlockSpec((width, columns), lambda g, rows: (rows[g], 0)),
            ],
            out_specs=[
                pl.BlockSpec((1, height, width), lambda g, rows: (jnp.minimum(g, half - 1), 0, 0)),
                pl.BlockSpec((1, height, width), lambda g, rows: (jnp.maximum(g - half, 0), 0, 0)),
            ],
            scratch_shapes=[pltpu.VMEM((height, columns), jnp.bfloat16)],
        ),
        out_shape=[result, result],
        cost_estimate=pl.CostEstimate(
            flops=2 * height * columns * width * count,
            bytes_accessed=2 * (height * columns + width * columns * count),
            transcendentals=0,
        ),
        name="project",
    )(rows, anomalies, gradient, basis)


def synthesize_kernel(levels, rows_ref, places_ref, *refs):
    blocks, (basis_ref, anomalies_ref, out_ref) = refs[:-3], refs[-3:]
    total = None
    for index, block in enumerate(blocks):
        width = block.shape[1]
        rows = basis_ref[pl.ds(rows_ref[index] * width, width), :]
        term = jnp.dot(block[...], rows, preferred_element_type=jnp.float32)
        total = term if total is None else total + term
    result = None
    for member in range(anomalies_ref.shape[0]):
        term = anomalies_ref[member].astype(jnp.float32) * total[member * levels : (member + 1) * levels]
        result = term if result is None else result + term
    out_ref[0] = result


def synthesize(blocks, basis, anomalies, rows, places, parts, tile):
    members, levels, columns = anomalies.shape
    piece = columns // parts
    steps = piece // tile
    count = places.shape[0]
    block_spec = pl.BlockSpec(blocks[0].shape, lambda p, t, rows, places: (0, 0))
    return pl.pallas_call(
        lambda *refs: synthesize_kernel(levels, *refs),
        grid_spec=pltpu.PrefetchScalarGridSpec(
            num_scalar_prefetch=2,
            grid=(count, steps),
            in_specs=[block_spec] * len(blocks)
            + [
                pl.BlockSpec((basis.shape[0], tile), lambda p, t, rows, places: (0, places[p] * steps + t)),
                pl.BlockSpec((members, levels, tile), lambda p, t, rows, places: (0, 0, places[p] * steps + t)),
            ],
            out_specs=pl.BlockSpec((1, levels, tile), lambda p, t, rows, places: (p, 0, t)),
        ),
        out_shape=jax.ShapeDtypeStruct((count, levels, piece), jnp.float32),
        cost_estimate=pl.CostEstimate(
            flops=2 * members * levels * basis.shape[0] * piece * count,
            bytes_accessed=2 * (basis.shape[0] + members * levels) * piece * count,
            transcendentals=0,
        ),
        name="synthesize",
    )(rows, places, *blocks, basis, anomalies)


def two_parts(value):
    high = lax.reduce_precision(value, 8, 7)
    return high.astype(jnp.bfloat16), (value - high).astype(jnp.bfloat16)


def mixing(values, row_ids, column_ids):
    levels = values.shape[0]
    same = row_ids[:, None] == column_ids[None, :]
    tiled = jnp.tile(values, (1, column_ids.shape[0] // levels))
    wide = jnp.tile(tiled, (row_ids.shape[0] // levels, 1))
    return [jnp.where(same, part, jnp.zeros((), jnp.bfloat16)) for part in two_parts(wide)]


def on_device(anomalies, alpha, basis, gradient, vertical_root, band_gain, band, order):
    bf16, f32 = jnp.bfloat16, jnp.float32
    mem_count, state_count = lax.axis_size("mem"), lax.axis_size("state")
    mem_rank, state_rank = lax.axis_index("mem"), lax.axis_index("state")
    member_dev, levels, columns = anomalies.shape
    width = alpha.shape[2]
    height = member_dev * levels
    pairs = state_count // 2
    spot, core = state_rank // 2, state_rank % 2

    def along_mem(value, step):
        return lax.ppermute(value, "mem", [(i, (i + step) % mem_count) for i in range(mem_count)])

    def across_pairs(value, step):
        return lax.ppermute(
            value, "state", [(i, (i + 2 * step) % state_count) for i in range(state_count)]
        )

    def other_core(value):
        return lax.ppermute(value, "state", [(i, i ^ 1) for i in range(state_count)])

    def gather_mem(value):
        return jnp.concatenate([value] + [along_mem(value, step) for step in range(1, mem_count)], axis=0)

    slots = gather_mem(alpha.reshape(height, width))

    onehot = (band[:, None] == jnp.arange(band_gain.shape[0], dtype=jnp.int32)[None, :]).astype(f32)
    filter_gain = jnp.sum(onehot * band_gain[None, :], axis=1)
    sources = (mem_rank - jnp.arange(mem_count, dtype=jnp.int32)) % mem_count
    slot_members = order.reshape(mem_count, member_dev)
    held = (sources[:, None] * member_dev + jnp.arange(member_dev, dtype=jnp.int32)[None, :]).reshape(-1)
    own = mem_rank * member_dev + jnp.arange(member_dev, dtype=jnp.int32)
    spread = lambda ids: jnp.repeat(ids, levels)
    to_members = mixing(vertical_root, spread(own), spread(slot_members[sources].reshape(-1)))
    to_slots = mixing(vertical_root.T, spread(slot_members[mem_rank]), spread(held))

    targets = (spot + jnp.arange(pairs, dtype=jnp.int32)) % pairs
    given, kept = project(
        anomalies, gradient, basis, jnp.concatenate([2 * targets + 1 - core, 2 * targets + core]), width
    )
    taken = other_core(given)
    chip_sums = [kept[step] + taken[step] for step in range(pairs)]
    projected = chip_sums[0]
    arrived = [across_pairs(chip_sums[step].astype(bf16), step) for step in range(1, pairs)]
    for block in arrived:
        projected = projected + block.astype(f32)

    coef = sum(jnp.dot(part, slots, preferred_element_type=f32) for part in to_members)
    coef = (coef * filter_gain[None, :]).astype(bf16)
    own_core = [coef] + [across_pairs(coef, step) for step in range(1, pairs)]
    blocks = own_core + [other_core(block) for block in own_core]
    origins = (spot - jnp.arange(pairs, dtype=jnp.int32)) % pairs
    rows = jnp.concatenate([2 * origins + core, 2 * origins + 1 - core])
    tile = min(512, columns // mem_count)
    places = (mem_rank + jnp.arange(mem_count, dtype=jnp.int32)) % mem_count
    far = synthesize(blocks, basis, anomalies, rows, places[1:], mem_count, tile)
    piece_sum = synthesize(blocks, basis, anomalies, rows, places[:1], mem_count, tile)[0]
    shares = [along_mem(far[step - 1].astype(bf16), step) for step in range(1, mem_count)]
    for share in shares:
        piece_sum = piece_sum + share.astype(f32)
    summed = piece_sum.astype(bf16)
    all_pieces = jnp.stack([summed] + [along_mem(summed, step) for step in range(1, mem_count)])
    increment = jnp.concatenate(
        [all_pieces[(mem_rank - place) % mem_count] for place in range(mem_count)], axis=1
    ).astype(f32)

    member_projections = gather_mem(projected.astype(bf16))
    alpha_grad = sum(jnp.dot(part, member_projections, preferred_element_type=f32) for part in to_slots)
    alpha_grad = (alpha_grad * filter_gain[None, :]).reshape(member_dev, levels, width)
    return (increment, alpha_grad)


def solution(mesh):
    return jax.shard_map(
        on_device,
        mesh=mesh,
        in_specs=(
            P("mem", None, "state"),
            P("mem", None, "state"),
            P(None, "state"),
            P(None, "state"),
            P(),
            P(),
            P("state"),
            P(),
        ),
        out_specs=(P(None, "state"), P("mem", None, "state")),
        check_vma=False,
    )
```

time: 207 us -> 122 us (0.59)
  the two profiles are of different devices: /device:TPU:0 before, /device:TPU:9 now
where the time goes in v1:
time: 122 us
  waiting for transfers between devices  37.8 us (31%)
  Pallas kernels  36.7 us (30%)
  starting transfers between devices  26 us (21%)
  other arithmetic  11.8 us (10%)
  local copies, waits for them, and re-layouts  4.72 us (4%)
  matrix products  3.78 us (3%)
    ppermute x12, waiting for transfers between devices, along_mem(): lax.ppermute(value, 'mem', [(i, (i + step) % mem_count) for i in range(me...  23.2 us
    pallas_call x2, Pallas kernels, synthesize(): pl.pallas_call(lambda *refs: synthesize_kernel(levels, *refs), grid_spec=...  19.4 us
    pallas_call x1, Pallas kernels, project(): pl.pallas_call(project_kernel, grid_spec=pltpu.PrefetchScalarGridSpec(num...  17.3 us
    ppermute x6, waiting for transfers between devices, across_pairs(): lax.ppermute(value, 'state', [(i, (i + 2 * step) % state_count) for i in...  14.4 us
    ppermute x12, starting transfers between devices, along_mem(): lax.ppermute(value, 'mem', [(i, (i + step) % mem_count) for i in range(me...  13 us
    ppermute x6, starting transfers between devices, across_pairs(): lax.ppermute(value, 'state', [(i, (i + 2 * step) % state_count) for i in...  7.24 us
    ppermute x5, starting transfers between devices, other_core(): lax.ppermute(value, 'state', [(i, i ^ 1) for i in range(state_count)])  5.8 us
  transfers between devices with their start and end apart: 23, of which 8 were waited for; matrix products, arithmetic and copies ran while one was open for 12% of the time, Pallas kernels for 30%

profile of v1, /device:TPU:9, one launch (start us, length us, event | category | flops | bytes accessed | tf_op | source)
XLA Modules:
  0.0 121.8 jit_solution(930749933243244709)
XLA Ops:
  0.6 1.3 %collective-permute-start = (bf16[512,256]{1,0:T(8,128)(2,1)}, bf16[512,256]{1,0:T(8,128)(2,1)S(1)}, u32[]{:S(2)}, u32[]{:S(2)}) collective-permute-start(bf16[512,256]{1,0:T(8,128)(2,1)} %bitcast.78), channel_id=1, source_target_pairs={{0,8},{8,16},{16,24},{24,0},{1,9},{9,17},{17,25},{25,1},{2,10},{10... | collective-permute-start | bytes 786440 | tf_op jit(solution)/shard_map/ppermute | solution.py:134
  2.0 1.1 collective-permute-start.1
  3.1 1.4 %collective-permute-start.2 = (bf16[512,256]{1,0:T(8,128)(2,1)}, bf16[512,256]{1,0:T(8,128)(2,1)S(1)}, u32[]{:S(2)}, u32[]{:S(2)}) collective-permute-start(bf16[512,256]{1,0:T(8,128)(2,1)} %bitcast.80), channel_id=1, source_target_pairs={{0,24},{8,0},{16,8},{24,16},{1,25},{9,1},{17,9},{25,17},{2,26},{10... | collective-permute-start | bytes 786440 | tf_op jit(solution)/shard_map/ppermute | solution.py:134
  5.1 17.3 %project.1 = (f32[4,512,256]{2,1,0:T(8,128)}, f32[4,512,256]{2,1,0:T(8,128)}) custom-call(s32[8]{0:T(128)} %pad_add_fusion.1.rows_ref, bf16[16,32,4096]{2,1,0:T(8,128)(2,1)} %anomalies_ref.1, bf16[32,4096]{1,0:T(8,128)(2,1)} %gradient_ref.1, bf16[2048,4096]{1,0:T(8,128)(2,1)} %basis_ref.1), custom_call_target="tpu_custom_call" | custom-call | flops 8589934592 | bytes 20971520 | tf_op jit(solution)/shard_map/project/pallas_call | solution.py:41
  22.4 1.5 %collective-permute-start.16 = (f32[4,512,256]{2,1,0:T(8,128)}, f32[4,512,256]{2,1,0:T(8,128)}, u32[]{:S(2)}, u32[]{:S(2)}) collective-permute-start(f32[4,512,256]{2,1,0:T(8,128)} %get-tuple-element.5), channel_id=1, source_target_pairs={{0,1},{1,0},{2,3},{3,2},{4,5},{5,4},{6,7},{7,6},{8,9},{9,8},{10,11... | collective-permute-start | bytes 6291464 | tf_op jit(solution)/shard_map/ppermute | solution.py:142
  28.4 1.3 %collective-permute-start.3 = (bf16[512,256]{1,0:T(8,128)(2,1)S(1)}, bf16[512,256]{1,0:T(8,128)(2,1)S(1)}, u32[]{:S(2)}, u32[]{:S(2)}) collective-permute-start(bf16[512,256]{1,0:T(8,128)(2,1)S(1)} %fusion.14.refs_2_), channel_id=1, source_target_pairs={{0,2},{1,3},{2,4},{3,5},{4,6},{5,7},{6,0},{7,1},{8,10},{9,11},{10,... | collective-permute-start | bytes 786440 | tf_op jit(solution)/shard_map/ppermute | solution.py:137
  29.7 1.2 %collective-permute-start.4 = (bf16[512,256]{1,0:T(8,128)(2,1)S(1)}, bf16[512,256]{1,0:T(8,128)(2,1)S(1)}, u32[]{:S(2)}, u32[]{:S(2)}) collective-permute-start(bf16[512,256]{1,0:T(8,128)(2,1)S(1)} %fusion.14.refs_2_), channel_id=1, source_target_pairs={{0,4},{1,5},{2,6},{3,7},{4,0},{5,1},{6,2},{7,3},{8,12},{9,13},{10,... | collective-permute-start | bytes 786440 | tf_op jit(solution)/shard_map/ppermute | solution.py:137
  30.9 1.1 collective-permute-start.5
  32.1 1.4 %collective-permute-start.6 = (bf16[512,256]{1,0:T(8,128)(2,1)S(1)}, bf16[512,256]{1,0:T(8,128)(2,1)S(1)}, u32[]{:S(2)}, u32[]{:S(2)}) collective-permute-start(bf16[512,256]{1,0:T(8,128)(2,1)S(1)} %fusion.14.refs_2_), channel_id=1, source_target_pairs={{0,1},{1,0},{2,3},{3,2},{4,5},{5,4},{6,7},{7,6},{8,9},{9,8},{10,11... | collective-permute-start | bytes 786440 | tf_op jit(solution)/shard_map/ppermute | solution.py:142
  33.5 3.3 %collective-permute-done.3.refs_3_ = bf16[512,256]{1,0:T(8,128)(2,1)S(1)} collective-permute-done((bf16[512,256]{1,0:T(8,128)(2,1)S(1)}, bf16[512,256]{1,0:T(8,128)(2,1)S(1)}, u32[]{:S(2)}, u32[]{:S(2)}) %collective-permute-start.3) | collective-permute-done | bytes 262176 | tf_op jit(solution)/shard_map/ppermute | solution.py:137
  36.8 2.3 %collective-permute-start.7 = (bf16[512,256]{1,0:T(8,128)(2,1)S(1)}, bf16[512,256]{1,0:T(8,128)(2,1)S(1)}, u32[]{:S(2)}, u32[]{:S(2)}) collective-permute-start(bf16[512,256]{1,0:T(8,128)(2,1)S(1)} %collective-permute-done.3.refs_3_), channel_id=1, source_target_pairs={{0,1},{1,0},{2,3},{3,2},{4,5},{5,4},{6,7},{7,6},{8,9},{9,8},{10,11... | collective-permute-start | bytes 786440 | tf_op jit(solution)/shard_map/ppermute | solution.py:142
  39.1 4.1 %collective-permute-done.4.refs_4_ = bf16[512,256]{1,0:T(8,128)(2,1)S(1)} collective-permute-done((bf16[512,256]{1,0:T(8,128)(2,1)S(1)}, bf16[512,256]{1,0:T(8,128)(2,1)S(1)}, u32[]{:S(2)}, u32[]{:S(2)}) %collective-permute-start.4) | collective-permute-done | bytes 262176 | tf_op jit(solution)/shard_map/ppermute | solution.py:137
  46.7 12.4 %synthesize.3 = f32[3,32,1024]{2,1,0:T(8,128)} custom-call(s32[8]{0:T(128)} %pad_add_fusion.refs_0_, s32[3]{0:T(128)} %slice.43.refs_1_, bf16[512,256]{1,0:T(8,128)(2,1)} %copy-done.2, bf16[512,256]{1,0:T(8,128)(2,1)} %copy-done.3, bf16[512,256]{1,0:T(8,128)(2,1)} %copy-done.4, bf16[512,256]{1,0:T(8,128)(2,1)} %copy-done.5, bf16[512,256]{1,0:T(8,128)(2,1)} %copy-done.6, ...), custom_call_target="tpu_custom_call" | custom-call | flops 6442450944 | bytes 15728640 | tf_op jit(solution)/shard_map/synthesize/pallas_call | solution.py:88
  59.1 1.0 convert.5
  60.2 2.8 %collective-permute-start.11 = (bf16[32,1024]{1,0:T(8,128)(2,1)S(1)}, bf16[32,1024]{1,0:T(8,128)(2,1)S(1)}, u32[]{:S(2)}, u32[]{:S(2)}) collective-permute-start(bf16[32,1024]{1,0:T(8,128)(2,1)S(1)} %get-tuple-element.15), channel_id=1, source_target_pairs={{0,16},{8,24},{16,0},{24,8},{1,17},{9,25},{17,1},{25,9},{2,18},{10... | collective-permute-start | bytes 196616 | tf_op jit(solution)/shard_map/ppermute | solution.py:134
  63.0 7.0 %synthesize.2 = f32[1,32,1024]{2,1,0:T(8,128)} custom-call(s32[8]{0:T(128)} %pad_add_fusion.refs_0_, s32[1]{0:T(128)} %bitcast.77, bf16[512,256]{1,0:T(8,128)(2,1)} %copy-done.2, bf16[512,256]{1,0:T(8,128)(2,1)} %copy-done.3, bf16[512,256]{1,0:T(8,128)(2,1)} %copy-done.4, bf16[512,256]{1,0:T(8,128)(2,1)} %copy-done.5, bf16[512,256]{1,0:T(8,128)(2,1)} %copy-done.6, ...), custom_call_target="tpu_custom_call" | custom-call | flops 2147483648 | bytes 5242880 | tf_op jit(solution)/shard_map/synthesize/pallas_call | solution.py:88
  70.1 0.9 fusion.32
  71.0 1.2 %collective-permute-start.15 = (bf16[32,1024]{1,0:T(8,128)(2,1)S(1)}, bf16[32,1024]{1,0:T(8,128)(2,1)S(1)}, u32[]{:S(2)}, u32[]{:S(2)}) collective-permute-start(bf16[32,1024]{1,0:T(8,128)(2,1)S(1)} %fusion.32), channel_id=1, source_target_pairs={{0,24},{8,0},{16,8},{24,16},{1,25},{9,1},{17,9},{25,17},{2,26},{10... | collective-permute-start | bytes 196616 | tf_op jit(solution)/shard_map/ppermute | solution.py:134
  72.6 2.7 %collective-permute-start.14 = (bf16[32,1024]{1,0:T(8,128)(2,1)S(1)}, bf16[32,1024]{1,0:T(8,128)(2,1)}, u32[]{:S(2)}, u32[]{:S(2)}) collective-permute-start(bf16[32,1024]{1,0:T(8,128)(2,1)S(1)} %fusion.32), channel_id=1, source_target_pairs={{0,16},{8,24},{16,0},{24,8},{1,17},{9,25},{17,1},{25,9},{2,18},{10... | collective-permute-start | bytes 196616 | tf_op jit(solution)/shard_map/ppermute | solution.py:134
  75.4 2.3 %fusion.25 = (bf16[512,256]{1,0:T(8,128)(2,1)}, bf16[512,256]{1,0:T(8,128)(2,1)S(1)}, bf16[512,256]{1,0:T(8,128)(2,1)}) fusion(f32[4,512,256]{2,1,0:T(8,128)} %collective-permute-done.16, f32[4,512,256]{2,1,0:T(8,128)S(1)} %copy-done.1), kind=kLoop, calls=%fused_computation.40 | loop fusion | flops 786432 | bytes 3932160 | tf_op jit(solution)/shard_map/convert_element_type | solution.py:166
  77.7 1.5 %collective-permute-start.17 = (bf16[512,256]{1,0:T(8,128)(2,1)}, bf16[512,256]{1,0:T(8,128)(2,1)S(1)}, u32[]{:S(2)}, u32[]{:S(2)}) collective-permute-start(bf16[512,256]{1,0:T(8,128)(2,1)} %get-tuple-element.6), channel_id=1, source_target_pairs={{0,2},{1,3},{2,4},{3,5},{4,6},{5,7},{6,0},{7,1},{8,10},{9,11},{10,... | collective-permute-start | bytes 786440 | tf_op jit(solution)/shard_map/ppermute | solution.py:137
  79.4 1.9 %collective-permute-start.19 = (bf16[512,256]{1,0:T(8,128)(2,1)S(1)}, bf16[512,256]{1,0:T(8,128)(2,1)S(1)}, u32[]{:S(2)}, u32[]{:S(2)}) collective-permute-start(bf16[512,256]{1,0:T(8,128)(2,1)S(1)} %get-tuple-element.7), channel_id=1, source_target_pairs={{0,6},{1,7},{2,0},{3,1},{4,2},{5,3},{6,4},{7,5},{8,14},{9,15},{10,... | collective-permute-start | bytes 786440 | tf_op jit(solution)/shard_map/ppermute | solution.py:137
  82.6 1.9 %compare_select_fusion = bf16[512,2048]{1,0:T(8,128)(2,1)} fusion(f32[32,2048]{1,0:T(8,128)S(1)} %tile.37, s32[2048]{0:T(1024)S(1)} %eq.68, s32[512]{0:T(512)S(1)} %eq.66), kind=kLoop, calls=%fused_computation.7 | loop fusion | flops 5242880 | bytes 2369536 | tf_op jit(solution)/shard_map/jit(_where)/select_n | solution.py:120
  84.5 1.1 pad_maximum_fusion.2
  85.6 6.9 %collective-permute-done.18 = bf16[512,256]{1,0:T(8,128)(2,1)S(1)} collective-permute-done((bf16[512,256]{1,0:T(8,128)(2,1)}, bf16[512,256]{1,0:T(8,128)(2,1)S(1)}, u32[]{:S(2)}, u32[]{:S(2)}) %collective-permute-start.18) | collective-permute-done | bytes 262176 | tf_op jit(solution)/shard_map/ppermute | solution.py:137
  92.5 1.3 %fusion.24 = bf16[512,256]{1,0:T(8,128)(2,1)S(1)} fusion(f32[4,512,256]{2,1,0:T(8,128)} %collective-permute-done.16, bf16[512,256]{1,0:T(8,128)(2,1)S(1)} %collective-permute-done.19, bf16[512,256]{1,0:T(8,128)(2,1)S(1)} %collective-permute-done.18, bf16[512,256]{1,0:T(8,128)(2,1)S(1)} %collective-permute-done.17, f32[4,512,256]{2,1,0:T(8,128)} %get-tuple-element.4), kind=kLoop, calls=%fused_computation.39 | loop fusion | flops 1048576 | bytes 2097152 | tf_op jit(solution)/shard_map/convert_element_type | solution.py:189
  93.9 1.9 %collective-permute-start.21 = (bf16[512,256]{1,0:T(8,128)(2,1)S(1)}, bf16[512,256]{1,0:T(8,128)(2,1)S(1)}, u32[]{:S(2)}, u32[]{:S(2)}) collective-permute-start(bf16[512,256]{1,0:T(8,128)(2,1)S(1)} %fusion.24), channel_id=1, source_target_pairs={{0,16},{8,24},{16,0},{24,8},{1,17},{9,25},{17,1},{25,9},{2,18},{10... | collective-permute-start | bytes 786440 | tf_op jit(solution)/shard_map/ppermute | solution.py:134
  95.8 0.8 maximum_convert_fusion
  96.6 4.4 %collective-permute-done.20 = bf16[512,256]{1,0:T(8,128)(2,1)S(1)} collective-permute-done((bf16[512,256]{1,0:T(8,128)(2,1)S(1)}, bf16[512,256]{1,0:T(8,128)(2,1)S(1)}, u32[]{:S(2)}, u32[]{:S(2)}) %collective-permute-start.20) | collective-permute-done | bytes 262176 | tf_op jit(solution)/shard_map/ppermute | solution.py:134
  101.1 14.9 %collective-permute-done.21 = bf16[512,256]{1,0:T(8,128)(2,1)S(1)} collective-permute-done((bf16[512,256]{1,0:T(8,128)(2,1)S(1)}, bf16[512,256]{1,0:T(8,128)(2,1)S(1)}, u32[]{:S(2)}, u32[]{:S(2)}) %collective-permute-start.21) | collective-permute-done | bytes 262176 | tf_op jit(solution)/shard_map/ppermute | solution.py:134
  116.0 3.5 %collective-permute-done.22 = bf16[512,256]{1,0:T(8,128)(2,1)S(1)} collective-permute-done((bf16[512,256]{1,0:T(8,128)(2,1)S(1)}, bf16[512,256]{1,0:T(8,128)(2,1)S(1)}, u32[]{:S(2)}, u32[]{:S(2)}) %collective-permute-start.22) | collective-permute-done | bytes 262176 | tf_op jit(solution)/shard_map/ppermute | solution.py:134
  120.2 1.6 %fusion.11 = f32[512,256]{1,0:T(8,128)} fusion(f32[512,256]{1,0:T(8,128)S(1)} %fusion.28, bf16[512,2048]{1,0:T(8,128)(2,1)S(1)} %fusion.1, s32[2048]{0:T(1024)S(1)} %eq.68, s32[512]{0:T(512)S(1)} %eq.66, f32[256]{0:T(256)S(1)} %select_reduce_fusion, bf16[512,256]{1,0:T(8,128)(2,1)S(1)} %collective-permute-done.22, ...), kind=kOutput, calls=%fused_computation.20 | convolution fusion | flops 543424512 | bytes 4205568 | tf_op jit(solution)/shard_map/dot_general | solution.py:190
  (99 shorter events, 11.3 us)
Async XLA Ops:
  0.6 25.8 %collective-permute-start = (bf16[512,256]{1,0:T(8,128)(2,1)}, bf16[512,256]{1,0:T(8,128)(2,1)S(1)}, u32[]{:S(2)}, u32[]{:S(2)}) collective-permute-start(bf16[512,256]{1,0:T(8,128)(2,1)} %bitcast.78), channel_id=1, source_target_pairs={{0,8},{8,16},{16,24},{24,0},{1,9},{9,17},{17,25},{25,1},{2,10},{10... | collective-permute-start | bytes 786440 | tf_op jit(solution)/shard_map/ppermute | solution.py:134
  2.0 24.5 %collective-permute-start.1 = (bf16[512,256]{1,0:T(8,128)(2,1)}, bf16[512,256]{1,0:T(8,128)(2,1)S(1)}, u32[]{:S(2)}, u32[]{:S(2)}) collective-permute-start(bf16[512,256]{1,0:T(8,128)(2,1)} %bitcast.79), channel_id=1, source_target_pairs={{0,16},{8,24},{16,0},{24,8},{1,17},{9,25},{17,1},{25,9},{2,18},{10... | collective-permute-start | bytes 786440 | tf_op jit(solution)/shard_map/ppermute | solution.py:134
  3.1 23.8 %collective-permute-start.2 = (bf16[512,256]{1,0:T(8,128)(2,1)}, bf16[512,256]{1,0:T(8,128)(2,1)S(1)}, u32[]{:S(2)}, u32[]{:S(2)}) collective-permute-start(bf16[512,256]{1,0:T(8,128)(2,1)} %bitcast.80), channel_id=1, source_target_pairs={{0,24},{8,0},{16,8},{24,16},{1,25},{9,1},{17,9},{25,17},{2,26},{10... | collective-permute-start | bytes 786440 | tf_op jit(solution)/shard_map/ppermute | solution.py:134
  5.1 18.9 %copy-start.15 = (s32[64]{0:T(128)S(1)}, s32[64]{0:T(128)}, u32[]{:S(2)}) copy-start(s32[64]{0:T(128)} %param.15) | copy-start | bytes 772
  5.1 19.9 %copy-start.10 = (f32[32,32]{1,0:T(8,128)S(1)}, f32[32,32]{1,0:T(8,128)}, u32[]{:S(2)}) copy-start(f32[32,32]{1,0:T(8,128)} %param.12) | copy-start | bytes 12292
  22.4 53.0 %collective-permute-start.16 = (f32[4,512,256]{2,1,0:T(8,128)}, f32[4,512,256]{2,1,0:T(8,128)}, u32[]{:S(2)}, u32[]{:S(2)}) collective-permute-start(f32[4,512,256]{2,1,0:T(8,128)} %get-tuple-element.5), channel_id=1, source_target_pairs={{0,1},{1,0},{2,3},{3,2},{4,5},{5,4},{6,7},{7,6},{8,9},{9,8},{10,11... | collective-permute-start | bytes 6291464 | tf_op jit(solution)/shard_map/ppermute | solution.py:142
  28.4 16.8 %copy-start.2 = (bf16[512,256]{1,0:T(8,128)(2,1)}, bf16[512,256]{1,0:T(8,128)(2,1)S(1)}, u32[]{:S(2)}) copy-start(bf16[512,256]{1,0:T(8,128)(2,1)S(1)} %fusion.14.refs_2_) | copy-start | bytes 786436
  28.4 8.4 %collective-permute-start.3 = (bf16[512,256]{1,0:T(8,128)(2,1)S(1)}, bf16[512,256]{1,0:T(8,128)(2,1)S(1)}, u32[]{:S(2)}, u32[]{:S(2)}) collective-permute-start(bf16[512,256]{1,0:T(8,128)(2,1)S(1)} %fusion.14.refs_2_), channel_id=1, source_target_pairs={{0,2},{1,3},{2,4},{3,5},{4,6},{5,7},{6,0},{7,1},{8,10},{9,11},{10,... | collective-permute-start | bytes 786440 | tf_op jit(solution)/shard_map/ppermute | solution.py:137
  29.7 13.5 %collective-permute-start.4 = (bf16[512,256]{1,0:T(8,128)(2,1)S(1)}, bf16[512,256]{1,0:T(8,128)(2,1)S(1)}, u32[]{:S(2)}, u32[]{:S(2)}) collective-permute-start(bf16[512,256]{1,0:T(8,128)(2,1)S(1)} %fusion.14.refs_2_), channel_id=1, source_target_pairs={{0,4},{1,5},{2,6},{3,7},{4,0},{5,1},{6,2},{7,3},{8,12},{9,13},{10,... | collective-permute-start | bytes 786440 | tf_op jit(solution)/shard_map/ppermute | solution.py:137
  30.9 12.8 %collective-permute-start.5 = (bf16[512,256]{1,0:T(8,128)(2,1)S(1)}, bf16[512,256]{1,0:T(8,128)(2,1)S(1)}, u32[]{:S(2)}, u32[]{:S(2)}) collective-permute-start(bf16[512,256]{1,0:T(8,128)(2,1)S(1)} %fusion.14.refs_2_), channel_id=1, source_target_pairs={{0,6},{1,7},{2,0},{3,1},{4,2},{5,3},{6,4},{7,5},{8,14},{9,15},{10,... | collective-permute-start | bytes 786440 | tf_op jit(solution)/shard_map/ppermute | solution.py:137
  32.1 27.0 %copy-start.13 = (s32[4]{0:T(128)}, s32[4]{0:T(128)S(1)}, u32[]{:S(2)}) copy-start(s32[4]{0:T(128)S(1)} %get-tuple-element.16) | copy-start | bytes 52
  32.1 12.9 %collective-permute-start.6 = (bf16[512,256]{1,0:T(8,128)(2,1)S(1)}, bf16[512,256]{1,0:T(8,128)(2,1)S(1)}, u32[]{:S(2)}, u32[]{:S(2)}) collective-permute-start(bf16[512,256]{1,0:T(8,128)(2,1)S(1)} %fusion.14.refs_2_), channel_id=1, source_target_pairs={{0,1},{1,0},{2,3},{3,2},{4,5},{5,4},{6,7},{7,6},{8,9},{9,8},{10,11... | collective-permute-start | bytes 786440 | tf_op jit(solution)/shard_map/ppermute | solution.py:142
  36.8 8.5 %copy-start.3 = (bf16[512,256]{1,0:T(8,128)(2,1)}, bf16[512,256]{1,0:T(8,128)(2,1)S(1)}, u32[]{:S(2)}) copy-start(bf16[512,256]{1,0:T(8,128)(2,1)S(1)} %collective-permute-done.3.refs_3_) | copy-start | bytes 786436
  36.8 8.3 %collective-permute-start.7 = (bf16[512,256]{1,0:T(8,128)(2,1)S(1)}, bf16[512,256]{1,0:T(8,128)(2,1)S(1)}, u32[]{:S(2)}, u32[]{:S(2)}) collective-permute-start(bf16[512,256]{1,0:T(8,128)(2,1)S(1)} %collective-permute-done.3.refs_3_), channel_id=1, source_target_pairs={{0,1},{1,0},{2,3},{3,2},{4,5},{5,4},{6,7},{7,6},{8,9},{9,8},{10,11... | collective-permute-start | bytes 786440 | tf_op jit(solution)/shard_map/ppermute | solution.py:142
  43.2 1.9 %collective-permute-start.8 = (bf16[512,256]{1,0:T(8,128)(2,1)S(1)}, bf16[512,256]{1,0:T(8,128)(2,1)S(1)}, u32[]{:S(2)}, u32[]{:S(2)}) collective-permute-start(bf16[512,256]{1,0:T(8,128)(2,1)S(1)} %collective-permute-done.4.refs_4_), channel_id=1, source_target_pairs={{0,1},{1,0},{2,3},{3,2},{4,5},{5,4},{6,7},{7,6},{8,9},{9,8},{10,11... | collective-permute-start | bytes 786440 | tf_op jit(solution)/shard_map/ppermute | solution.py:142
  43.7 1.5 %collective-permute-start.9 = (bf16[512,256]{1,0:T(8,128)(2,1)S(1)}, bf16[512,256]{1,0:T(8,128)(2,1)S(1)}, u32[]{:S(2)}, u32[]{:S(2)}) collective-permute-start(bf16[512,256]{1,0:T(8,128)(2,1)S(1)} %collective-permute-done.5.refs_5_), channel_id=1, source_target_pairs={{0,1},{1,0},{2,3},{3,2},{4,5},{5,4},{6,7},{7,6},{8,9},{9,8},{10,11... | collective-permute-start | bytes 786440 | tf_op jit(solution)/shard_map/ppermute | solution.py:142
  60.1 9.9 %collective-permute-start.10 = (bf16[32,1024]{1,0:T(8,128)(2,1)S(1)}, bf16[32,1024]{1,0:T(8,128)(2,1)S(1)}, u32[]{:S(2)}, u32[]{:S(2)}) collective-permute-start(bf16[32,1024]{1,0:T(8,128)(2,1)S(1)} %get-tuple-element.13), channel_id=1, source_target_pairs={{0,8},{8,16},{16,24},{24,0},{1,9},{9,17},{17,25},{25,1},{2,10},{10... | collective-permute-start | bytes 196616 | tf_op jit(solution)/shard_map/ppermute | solution.py:134
  60.2 9.9 %collective-permute-start.11 = (bf16[32,1024]{1,0:T(8,128)(2,1)S(1)}, bf16[32,1024]{1,0:T(8,128)(2,1)S(1)}, u32[]{:S(2)}, u32[]{:S(2)}) collective-permute-start(bf16[32,1024]{1,0:T(8,128)(2,1)S(1)} %get-tuple-element.15), channel_id=1, source_target_pairs={{0,16},{8,24},{16,0},{24,8},{1,17},{9,25},{17,1},{25,9},{2,18},{10... | collective-permute-start | bytes 196616 | tf_op jit(solution)/shard_map/ppermute | solution.py:134
  63.0 7.1 %collective-permute-start.12 = (bf16[32,1024]{1,0:T(8,128)(2,1)S(1)}, bf16[32,1024]{1,0:T(8,128)(2,1)S(1)}, u32[]{:S(2)}, u32[]{:S(2)}) collective-permute-start(bf16[32,1024]{1,0:T(8,128)(2,1)S(1)} %get-tuple-element.14), channel_id=1, source_target_pairs={{0,24},{8,0},{16,8},{24,16},{1,25},{9,1},{17,9},{25,17},{2,26},{10... | collective-permute-start | bytes 196616 | tf_op jit(solution)/shard_map/ppermute | solution.py:134
  63.0 12.3 %copy-start.1 = (f32[4,512,256]{2,1,0:T(8,128)S(1)}, f32[4,512,256]{2,1,0:T(8,128)}, u32[]{:S(2)}) copy-start(f32[4,512,256]{2,1,0:T(8,128)} %get-tuple-element.4) | copy-start | bytes 6291460
  71.0 8.4 %collective-permute-start.15 = (bf16[32,1024]{1,0:T(8,128)(2,1)S(1)}, bf16[32,1024]{1,0:T(8,128)(2,1)S(1)}, u32[]{:S(2)}, u32[]{:S(2)}) collective-permute-start(bf16[32,1024]{1,0:T(8,128)(2,1)S(1)} %fusion.32), channel_id=1, source_target_pairs={{0,24},{8,0},{16,8},{24,16},{1,25},{9,1},{17,9},{25,17},{2,26},{10... | collective-permute-start | bytes 196616 | tf_op jit(solution)/shard_map/ppermute | solution.py:134
  72.3 12.2 %collective-permute-start.13 = (bf16[32,1024]{1,0:T(8,128)(2,1)S(1)}, bf16[32,1024]{1,0:T(8,128)(2,1)}, u32[]{:S(2)}, u32[]{:S(2)}) collective-permute-start(bf16[32,1024]{1,0:T(8,128)(2,1)S(1)} %fusion.32), channel_id=1, source_target_pairs={{0,8},{8,16},{16,24},{24,0},{1,9},{9,17},{17,25},{25,1},{2,10},{10... | collective-permute-start | bytes 196616 | tf_op jit(solution)/shard_map/ppermute | solution.py:134
  72.6 11.8 %collective-permute-start.14 = (bf16[32,1024]{1,0:T(8,128)(2,1)S(1)}, bf16[32,1024]{1,0:T(8,128)(2,1)}, u32[]{:S(2)}, u32[]{:S(2)}) collective-permute-start(bf16[32,1024]{1,0:T(8,128)(2,1)S(1)} %fusion.32), channel_id=1, source_target_pairs={{0,16},{8,24},{16,0},{24,8},{1,17},{9,25},{17,1},{25,9},{2,18},{10... | collective-permute-start | bytes 196616 | tf_op jit(solution)/shard_map/ppermute | solution.py:134
  77.7 7.9 %collective-permute-start.17 = (bf16[512,256]{1,0:T(8,128)(2,1)}, bf16[512,256]{1,0:T(8,128)(2,1)S(1)}, u32[]{:S(2)}, u32[]{:S(2)}) collective-permute-start(bf16[512,256]{1,0:T(8,128)(2,1)} %get-tuple-element.6), channel_id=1, source_target_pairs={{0,2},{1,3},{2,4},{3,5},{4,6},{5,7},{6,0},{7,1},{8,10},{9,11},{10,... | collective-permute-start | bytes 786440 | tf_op jit(solution)/shard_map/ppermute | solution.py:137
  79.2 13.3 %collective-permute-start.18 = (bf16[512,256]{1,0:T(8,128)(2,1)}, bf16[512,256]{1,0:T(8,128)(2,1)S(1)}, u32[]{:S(2)}, u32[]{:S(2)}) collective-permute-start(bf16[512,256]{1,0:T(8,128)(2,1)} %get-tuple-element.8), channel_id=1, source_target_pairs={{0,4},{1,5},{2,6},{3,7},{4,0},{5,1},{6,2},{7,3},{8,12},{9,13},{10,... | collective-permute-start | bytes 786440 | tf_op jit(solution)/shard_map/ppermute | solution.py:137
  79.4 2.3 %copy-start.11 = (bf16[32,1024]{1,0:T(8,128)(2,1)}, bf16[32,1024]{1,0:T(8,128)(2,1)S(1)}, u32[]{:S(2)}) copy-start(bf16[32,1024]{1,0:T(8,128)(2,1)S(1)} %collective-permute-done.15) | copy-start | bytes 196612
  79.4 13.1 %collective-permute-start.19 = (bf16[512,256]{1,0:T(8,128)(2,1)S(1)}, bf16[512,256]{1,0:T(8,128)(2,1)S(1)}, u32[]{:S(2)}, u32[]{:S(2)}) collective-permute-start(bf16[512,256]{1,0:T(8,128)(2,1)S(1)} %get-tuple-element.7), channel_id=1, source_target_pairs={{0,6},{1,7},{2,0},{3,1},{4,2},{5,3},{6,4},{7,5},{8,14},{9,15},{10,... | collective-permute-start | bytes 786440 | tf_op jit(solution)/shard_map/ppermute | solution.py:137
  82.3 2.2 %copy-start.12 = (bf16[32,1024]{1,0:T(8,128)(2,1)S(1)}, bf16[32,1024]{1,0:T(8,128)(2,1)}, u32[]{:S(2)}) copy-start(bf16[32,1024]{1,0:T(8,128)(2,1)} %copy-done.11) | copy-start | bytes 196612
  84.4 35.0 %copy-start = (bf16[512,2048]{1,0:T(8,128)(2,1)S(1)}, bf16[512,2048]{1,0:T(8,128)(2,1)}, u32[]{:S(2)}) copy-start(bf16[512,2048]{1,0:T(8,128)(2,1)} %compare_select_fusion) | copy-start | bytes 6291460
  93.8 7.2 %collective-permute-start.20 = (bf16[512,256]{1,0:T(8,128)(2,1)S(1)}, bf16[512,256]{1,0:T(8,128)(2,1)S(1)}, u32[]{:S(2)}, u32[]{:S(2)}) collective-permute-start(bf16[512,256]{1,0:T(8,128)(2,1)S(1)} %fusion.24), channel_id=1, source_target_pairs={{0,8},{8,16},{16,24},{24,0},{1,9},{9,17},{17,25},{25,1},{2,10},{10... | collective-permute-start | bytes 786440 | tf_op jit(solution)/shard_map/ppermute | solution.py:134
  93.9 22.1 %collective-permute-start.21 = (bf16[512,256]{1,0:T(8,128)(2,1)S(1)}, bf16[512,256]{1,0:T(8,128)(2,1)S(1)}, u32[]{:S(2)}, u32[]{:S(2)}) collective-permute-start(bf16[512,256]{1,0:T(8,128)(2,1)S(1)} %fusion.24), channel_id=1, source_target_pairs={{0,16},{8,24},{16,0},{24,8},{1,17},{9,25},{17,1},{25,9},{2,18},{10... | collective-permute-start | bytes 786440 | tf_op jit(solution)/shard_map/ppermute | solution.py:134
  95.8 23.7 %collective-permute-start.22 = (bf16[512,256]{1,0:T(8,128)(2,1)S(1)}, bf16[512,256]{1,0:T(8,128)(2,1)S(1)}, u32[]{:S(2)}, u32[]{:S(2)}) collective-permute-start(bf16[512,256]{1,0:T(8,128)(2,1)S(1)} %fusion.24), channel_id=1, source_target_pairs={{0,24},{8,0},{16,8},{24,16},{1,25},{9,1},{17,9},{25,17},{2,26},{10... | collective-permute-start | bytes 786440 | tf_op jit(solution)/shard_map/ppermute | solution.py:134
  (9 other events, 9.6 us)
